TPU v7x, 32 devices: a whole 2x2x4 slice. The times are simulated.
32 devices in a mesh: dp: 4 (over x, core), vocab: 8 (over z, y).
Axes of the slice: x: 2, y: 2, z: 4, core: 2. Of those that a mesh axis runs over, the one named last changes fastest.
Arguments:
- hidden: bfloat16 [1024, 2048], P('dp', 'vocab'), may hold values from -30 to 30
- table: bfloat16 [16000, 2048], P('vocab'), may hold values from -20 to 20
- targets: int32 [1024], P('dp'), may hold values from 0 to 15999
- input_ids: int32 [2048], P(('dp', 'vocab')), may hold values from 0 to 15999, as said below
- cotangent: bfloat16 [2048, 2048], P(('dp', 'vocab')), may hold values from -0.4375 to 0.4375
Outputs:
- token_loss: float32 [1024], P('dp')
- hidden_grad: bfloat16 [1024, 2048], P('dp', 'vocab')
- table_grad: bfloat16 [16000, 2048], P('vocab', 'dp')
Inputs may be any that keep to these rules, and one draw needn't show every extreme that they name: `input_ids`: within the 64 rows of one device, at most 16 ids fall in any one block of 2000 consecutive ids (the rows of one index of vocab); in every draw some block receives exactly 16 ids from every device.
All inputs are finite; a program needn't handle non-finite values.
Results may differ from a plain program's by a relative error of at most 0.0034.
Values may be sent and summed in bfloat16 or wider, within the bound.
A program may use at most 128 MiB of HBM per device.

v0:
```python
import jax
import jax.numpy as jnp
from jax import lax
from jax.sharding import PartitionSpec as P


def body(hidden, table, targets, input_ids, cotangent):
    vocab_rows = table.shape[0]
    model_width = table.shape[1]
    data_count = lax.axis_size("dp")
    vocab_count = lax.axis_size("vocab")
    first_row = lax.axis_index("vocab") * vocab_rows
    hidden_full = lax.all_gather(hidden, "vocab", axis=1, tiled=True)
    logits = lax.dot_general(
        hidden_full, table, (((1,), (1,)), ((), ())), preferred_element_type=jnp.float32
    )
    columns = lax.broadcasted_iota(jnp.int32, logits.shape, 1)
    is_target = columns == (targets - first_row)[:, None]
    picked = jnp.sum(jnp.where(is_target, logits, 0.0), axis=1)
    local_max = jnp.max(logits, axis=1)
    row_max = lax.pmax(local_max, "vocab")
    shifted = jnp.exp(logits - row_max[:, None])
    row_sum, target_logit = lax.psum((jnp.sum(shifted, axis=1), picked), "vocab")
    token_loss = row_max + jnp.log(row_sum) - target_logit
    residual = (shifted / row_sum[:, None] - jnp.where(is_target, 1.0, 0.0)).astype(jnp.bfloat16)
    hidden_part = jnp.dot(residual, table, preferred_element_type=jnp.float32)
    hidden_grad = lax.psum_scatter(hidden_part, "vocab", scatter_dimension=1, tiled=True).astype(
        jnp.bfloat16
    )
    row_count = input_ids.shape[0]
    capacity = max(2, 2 * row_count // vocab_count)
    slot_total = vocab_count * capacity
    owners = input_ids // vocab_rows
    offsets = input_ids - owners * vocab_rows
    later_rows = lax.broadcasted_iota(jnp.int32, (row_count, row_count), 0)
    earlier_rows = lax.broadcasted_iota(jnp.int32, (row_count, row_count), 1)
    earlier = (owners[:, None] == owners[None, :]) & (earlier_rows < later_rows)
    position = jnp.sum(earlier.astype(jnp.int32), axis=1)
    slot_index = owners * capacity + position
    selector = lax.broadcasted_iota(jnp.int32, (slot_total, row_count), 0) == slot_index[None, :]
    send_rows = jnp.dot(
        selector.astype(jnp.bfloat16), cotangent, preferred_element_type=jnp.float32
    ).astype(jnp.bfloat16)
    send_rows = send_rows.reshape(vocab_count, capacity, model_width)
    send_offsets = jnp.sum(jnp.where(selector, offsets[None, :] + 1, 0), axis=1) - 1
    offset_copies = jnp.broadcast_to(
        send_offsets.reshape(vocab_count, capacity, 1), (vocab_count, capacity, data_count)
    )
    got_rows, got_offsets = (
        lax.all_to_all(
            lax.all_to_all(send_rows, "dp", split_axis=2, concat_axis=1, tiled=True),
            "vocab",
            split_axis=0,
            concat_axis=0,
            tiled=True,
        ),
        lax.all_to_all(
            lax.all_to_all(offset_copies, "dp", split_axis=2, concat_axis=1, tiled=True),
            "vocab",
            split_axis=0,
            concat_axis=0,
            tiled=True,
        ),
    )
    block_width = model_width // data_count
    flat_rows = got_rows.reshape(-1, block_width)
    flat_offsets = got_offsets.reshape(-1)
    matches = (
        lax.broadcasted_iota(jnp.int32, (vocab_rows, flat_offsets.shape[0]), 0)
        == flat_offsets[None, :]
    )
    start_sum = jnp.dot(matches.astype(jnp.bfloat16), flat_rows, preferred_element_type=jnp.float32)
    hidden_block = lax.all_to_all(hidden_full, "dp", split_axis=1, concat_axis=0, tiled=True)
    table_sum = start_sum + lax.dot_general(
        lax.all_gather(residual, "dp", axis=0, tiled=True),
        hidden_block,
        (((0,), (0,)), ((), ())),
        preferred_element_type=jnp.float32,
    )
    return (token_loss, hidden_grad, table_sum.astype(jnp.bfloat16))


def solution(mesh):
    placed = (
        P("dp", "vocab"),
        P("vocab", None),
        P("dp"),
        P(("dp", "vocab")),
        P(("dp", "vocab"), None),
    )
    return jax.shard_map(
        body,
        mesh=mesh,
        in_specs=placed,
        out_specs=(P("dp"), P("dp", "vocab"), P("vocab", "dp")),
        check_vma=False,
    )
```

profile of v0, /device:TPU:0, one launch (start us, length us, event | category | flops | bytes accessed | tf_op | source)
XLA Modules:
  0.0 228.6 jit_solution(13817739331604094054)
XLA Ops:
  7.2 0.0 copy-start
  7.2 0.0 all-gather.3.cloned.1.call-start
  7.2 1.7 copy.18
  8.9 0.0 all-gather.3.cloned.1.call-update
  8.9 0.0 reduce-scatter.2.cloned.1.call-start
  9.0 0.7 broadcast_subtract_fusion
  9.7 44.0 %all-gather.3.cloned.1.call-done = bf16[256,2048]{0,1:T(8,128)(2,1)} async-done(((bf16[256,256]{0,1:T(8,128)(2,1)}), bf16[256,2048]{0,1:T(8,128)(2,1)}) %all-gather.3.cloned.1.call-update) | async-done | bytes 1048592 | tf_op jit(solution)/shard_map/all_gather | solution.py:13
  53.7 5.9 %fusion.5 = (f32[256]{0:T(256)S(1)}, f32[256,2000]{0,1:T(8,128)S(1)}) fusion(bf16[2000,2048]{1,0:T(8,128)(2,1)} %param.6, bf16[256,2048]{0,1:T(8,128)(2,1)} %all-gather.3.cloned.1.call-done), kind=kOutput, calls=%fused_computation.22 | convolution fusion | flops 2097663744 | bytes 11289600 | tf_op jit(solution)/shard_map/dot_general | solution.py:14
  59.6 19.2 %pmax.7 = f32[256]{0:T(256)S(1)} all-reduce(f32[256]{0:T(256)S(1)} %get-tuple-element.9), channel_id=1, replica_groups=mesh['dp'=4,'vocab'=8] {'vocab'}, use_global_device_ids=true, to_apply=%region_1.2 | all-reduce | flops 256 | bytes 2048 | tf_op jit(solution)/shard_map/pmax | solution.py:21
  78.7 0.6 fusion.2
  79.3 17.1 %all-reduce = (f32[256]{0:T(256)S(1)}, f32[256]{0:T(256)S(1)}) all-reduce(f32[256]{0:T(256)S(1)} %get-tuple-element.4, f32[256]{0:T(256)S(1)} %get-tuple-element.3), channel_id=1, replica_groups=mesh['dp'=4,'vocab'=8] {'vocab'}, use_global_device_ids=true, to_apply=%region_5.6 | all-reduce | flops 512 | bytes 4096 | tf_op jit(solution)/shard_map/psum | solution.py:23
  96.4 0.6 subtract_convert_fusion
  97.0 0.0 copy-start.1
  97.0 7.4 %fusion.6 = f32[256,2048]{1,0:T(8,128)} fusion(bf16[256,2000]{0,1:T(8,128)(2,1)S(1)} %subtract_convert_fusion, bf16[2000,2048]{1,0:T(8,128)(2,1)} %param.6), kind=kOutput, calls=%fused_computation.25 | convolution fusion | flops 2097152000 | bytes 11313152 | tf_op jit(solution)/shard_map/dot_general | solution.py:26
  104.4 0.0 copy-done.1
  104.4 0.0 copy-start.2
  104.4 0.0 reduce-scatter.2.cloned.1.call-update
  104.5 0.0 all-gather.5.cloned.1.call-start
  104.5 0.7 all-gather.5.cloned.1.call-update
  105.2 0.0 copy-done.2
  105.2 0.2 convert_reduce_fusion
  105.4 0.1 select_reduce_fusion.1
  105.5 0.1 sub.44
  105.6 0.7 reshape.45
  106.3 3.2 %all-to-all-start = ((s32[4,1,128]{2,1,0:T(1,128)}), s32[4,1,128]{2,1,0:T(1,128)S(1)}, u32[]{:S(2)}, u32[]{:S(2)}) async-start(s32[4,1,128]{2,1,0:T(1,128)} %reshape.45), calls=%async_computation.1 | async-start | bytes 4096 | tf_op jit(solution)/shard_map/all_to_all | solution.py:58
  109.5 0.0 copy-done
  109.5 0.4 convolution_convert_fusion
  109.9 4.2 %copy.21 = bf16[8,16,2048]{1,0,2:T(8,128)(2,1)} copy(bf16[8,16,2048]{2,1,0:T(8,128)(2,1)S(1)} %bitcast.33) | data formatting | bytes 1048576 | tf_op jit(solution)/shard_map/reshape | solution.py:44
  114.1 6.5 %reshape.43 = bf16[4,2,32768]{2,1,0:T(2,128)(2,1)} reshape(bf16[2048,8,16]{2,1,0:T(8,128)(2,1)} %bitcast.30) | data formatting | bytes 1048576
  120.6 0.0 all-to-all-done
  120.6 3.5 %all-to-all-start.2 = ((bf16[4,2,32768]{2,1,0:T(2,128)(2,1)}), bf16[4,2,32768]{2,1,0:T(2,128)(2,1)S(1)}, u32[]{:S(2)}, u32[]{:S(2)}) async-start(bf16[4,2,32768]{2,1,0:T(2,128)(2,1)} %reshape.43), calls=%async_computation.3 | async-start | bytes 1048576 | tf_op jit(solution)/shard_map/all_to_all | solution.py:51
  124.1 0.5 broadcast.29
  124.6 0.7 reduce.4
  125.3 0.1 reshape.46
  125.4 0.7 all_to_all.49
  126.0 6.8 %all-to-all-done.2 = bf16[4,2,32768]{2,1,0:T(2,128)(2,1)S(1)} async-done(((bf16[4,2,32768]{2,1,0:T(2,128)(2,1)}), bf16[4,2,32768]{2,1,0:T(2,128)(2,1)S(1)}, u32[]{:S(2)}, u32[]{:S(2)}) %all-to-all-start.2) | async-done | bytes 524320 | tf_op jit(solution)/shard_map/all_to_all | solution.py:51
  132.9 3.3 %all-to-all-start.1 = ((s32[8,64,1]{1,2,0:T(1,128)}), s32[8,64,1]{1,2,0:T(1,128)S(1)}, u32[]{:S(2)}, u32[]{:S(2)}) async-start(s32[8,64,1]{1,2,0:T(1,128)} %bitcast.2), calls=%async_computation.2 | async-start | bytes 8192 | tf_op jit(solution)/shard_map/all_to_all | solution.py:57
  136.2 4.1 %reshape.44 = bf16[2048,8,16]{2,1,0:T(8,128)(2,1)} reshape(bf16[4,2,32768]{2,1,0:T(2,128)(2,1)S(1)} %all-to-all-done.2) | data formatting | bytes 1048576
  140.3 4.9 %copy.25 = bf16[8,16,4,512]{3,2,1,0:T(4,128)(2,1)S(1)} copy(bf16[8,16,4,512]{1,0,3,2:T(8,128)(2,1)} %bitcast.31) | data formatting | bytes 1048576 | tf_op jit(solution)/shard_map/all_to_all | solution.py:51
  145.2 0.1 copy.23
  145.3 0.0 all-to-all-done.1
  145.3 27.8 %all_to_all.65 = bf16[8,64,512]{2,1,0:T(8,128)(2,1)S(1)} all-to-all(bf16[8,64,512]{2,1,0:T(8,128)(2,1)S(1)} %bitcast.35), channel_id=1, replica_groups=mesh['dp'=4,'vocab'=8] {'vocab'}, dimensions={0} | all-to-all | bytes 1048576 | tf_op jit(solution)/shard_map/all_to_all | solution.py:50
  173.1 3.7 %all-to-all-start.4 = ((bf16[256,4,512]{0,2,1:T(8,128)(2,1)}), bf16[256,4,512]{0,2,1:T(8,128)(2,1)S(1)}, u32[]{:S(2)}, u32[]{:S(2)}) async-start(bf16[256,4,512]{0,2,1:T(8,128)(2,1)} %bitcast.8), calls=%async_computation.5 | async-start | bytes 2097152 | tf_op jit(solution)/shard_map/all_to_all | solution.py:73
  176.8 0.5 broadcast.27
  177.3 0.7 reduce.3
  178.0 0.1 eq.46
  178.1 3.1 %fusion = f32[2000,512]{1,0:T(8,128)} fusion(bf16[512,512]{1,0:T(8,128)(2,1)S(1)} %bitcast.37, s32[512]{0:T(512)S(1)} %eq.46), kind=kOutput, calls=%fused_computation.2 | convolution fusion | flops 1049600000 | bytes 4622336 | tf_op jit(solution)/shard_map/dot_general | solution.py:72
  181.2 0.6 add_subtract_fusion
  181.8 14.4 %all-to-all-done.4 = bf16[256,4,512]{0,2,1:T(8,128)(2,1)S(1)} async-done(((bf16[256,4,512]{0,2,1:T(8,128)(2,1)}), bf16[256,4,512]{0,2,1:T(8,128)(2,1)S(1)}, u32[]{:S(2)}, u32[]{:S(2)}) %all-to-all-start.4) | async-done | bytes 1048608 | tf_op jit(solution)/shard_map/all_to_all | solution.py:73
  196.1 0.5 copy.24
  196.7 0.0 reduce-scatter.2.cloned.1.call-done
  196.7 1.6 convert_element_type.18
  198.3 16.8 %all-gather.5.cloned.1.call-done = bf16[1024,2000]{0,1:T(8,128)(2,1)} async-done(((bf16[256,2000]{0,1:T(8,128)(2,1)}), bf16[1024,2000]{0,1:T(8,128)(2,1)}) %all-gather.5.cloned.1.call-update) | async-done | bytes 4096016 | tf_op jit(solution)/shard_map/all_gather | solution.py:75
  215.1 7.0 %add_convert_fusion = bf16[2000,512]{1,0:T(8,128)(2,1)} fusion(f32[2000,512]{1,0:T(8,128)} %fusion, bf16[1024,2000]{0,1:T(8,128)(2,1)} %all-gather.5.cloned.1.call-done, bf16[1024,512]{1,0:T(8,128)(2,1)S(1)} %bitcast.36), kind=kOutput, calls=%fused_computation | convolution fusion | flops 2099200000 | bytes 11288576 | tf_op jit(solution)/shard_map/dot_general | solution.py:74
  (6 shorter events, 0.0 us)
Async XLA Ops:
  7.2 102.4 %copy-start = (bf16[64,2048]{1,0:T(8,128)(2,1)S(1)}, bf16[64,2048]{1,0:T(8,128)(2,1)}, u32[]{:S(2)}) copy-start(bf16[64,2048]{1,0:T(8,128)(2,1)} %param.9) | copy-start | bytes 786436
  7.2 46.5 %all-gather.3.cloned.1.call-start = ((), (), s32[]{:S(2)}) async-start(), calls=%async_computation.6 | async-start | bytes 1179648 | tf_op jit(solution)/shard_map/all_gather | solution.py:13
  8.9 187.8 %reduce-scatter.2.cloned.1.call-start = ((), (), s32[]{:S(2)}) async-start(), calls=%async_computation.7 | async-start | bytes 2359296 | tf_op jit(solution)/shard_map/reduce_scatter | solution.py:27
  97.0 7.4 %copy-start.1 = (bf16[256,2000]{0,1:T(8,128)(2,1)}, bf16[256,2000]{0,1:T(8,128)(2,1)S(1)}, u32[]{:S(2)}) copy-start(bf16[256,2000]{0,1:T(8,128)(2,1)S(1)} %subtract_convert_fusion) | copy-start | bytes 3072004
  104.4 0.8 copy-start.2
  104.5 110.7 %all-gather.5.cloned.1.call-start = ((), (), s32[]{:S(2)}) async-start(), calls=%async_computation.8 | async-start | bytes 5120000 | tf_op jit(solution)/shard_map/all_gather | solution.py:75
  106.3 14.3 %all-to-all-start = ((s32[4,1,128]{2,1,0:T(1,128)}), s32[4,1,128]{2,1,0:T(1,128)S(1)}, u32[]{:S(2)}, u32[]{:S(2)}) async-start(s32[4,1,128]{2,1,0:T(1,128)} %reshape.45), calls=%async_computation.1 | async-start | bytes 4096 | tf_op jit(solution)/shard_map/all_to_all | solution.py:58
  120.6 12.3 %all-to-all-start.2 = ((bf16[4,2,32768]{2,1,0:T(2,128)(2,1)}), bf16[4,2,32768]{2,1,0:T(2,128)(2,1)S(1)}, u32[]{:S(2)}, u32[]{:S(2)}) async-start(bf16[4,2,32768]{2,1,0:T(2,128)(2,1)} %reshape.43), calls=%async_computation.3 | async-start | bytes 1048576 | tf_op jit(solution)/shard_map/all_to_all | solution.py:51
  132.9 12.5 %all-to-all-start.1 = ((s32[8,64,1]{1,2,0:T(1,128)}), s32[8,64,1]{1,2,0:T(1,128)S(1)}, u32[]{:S(2)}, u32[]{:S(2)}) async-start(s32[8,64,1]{1,2,0:T(1,128)} %bitcast.2), calls=%async_computation.2 | async-start | bytes 8192 | tf_op jit(solution)/shard_map/all_to_all | solution.py:57
  173.1 23.0 %all-to-all-start.4 = ((bf16[256,4,512]{0,2,1:T(8,128)(2,1)}), bf16[256,4,512]{0,2,1:T(8,128)(2,1)S(1)}, u32[]{:S(2)}, u32[]{:S(2)}) async-start(bf16[256,4,512]{0,2,1:T(8,128)(2,1)} %bitcast.8), calls=%async_computation.5 | async-start | bytes 2097152 | tf_op jit(solution)/shard_map/all_to_all | solution.py:73
Sparse Core Ops, SparseCore 0:
  10.7 42.9 all-gather.2
  104.6 70.6 reduce-scatter.1
  177.4 37.6 all-gather.4
where the time goes:
time: 229 us
  waiting for transfers between devices  82.8 us (36%)
  blocking collectives  64 us (28%)
  local copies, waits for them, and re-layouts  24.7 us (11%)
  matrix products  23.8 us (10%)
  between operations  13.9 us (6%)
  starting transfers between devices  13.8 us (6%)
  other arithmetic  5.64 us (2%)
    all_gather x1, waiting for transfers between devices, body(): hidden_full = lax.all_gather(hidden, 'vocab', axis=1, tiled=True)  44 us
    all_to_all x1, blocking collectives, body(): lax.all_to_all(lax.all_to_all(send_rows, 'dp', split_axis=2, concat_axis=...  27.8 us
    pmax x1, blocking collectives, body(): row_max = lax.pmax(local_max, 'vocab')  19.2 us
    psum x1, blocking collectives, body(): lax.psum((jnp.sum(shifted, axis=1), picked), 'vocab')  17.1 us
    all_gather x1, waiting for transfers between devices, body(): lax.all_gather(residual, 'dp', axis=0, tiled=True)  16.8 us
    all_to_all x1, waiting for transfers between devices, body(): lax.all_to_all(hidden_full, 'dp', split_axis=1, concat_axis=0, tiled=True)  14.4 us
    unnamed x12, local copies, waits for them, and re-layouts  13.1 us
    dot_general x1, matrix products, body(): hidden_part = jnp.dot(residual, table, preferred_element_type=jnp.float32)  7.42 us
  transfers between devices with their start and end apart: 7, of which 4 were waited for; matrix products, arithmetic and copies ran while one was open for 13% of the time, Pallas kernels for 0%

commit v1 on v0

--- a/solution.py
+++ b/solution.py
@@ -48,7 +48,12 @@
     )
     got_rows, got_offsets = (
         lax.all_to_all(
-            lax.all_to_all(send_rows, "dp", split_axis=2, concat_axis=1, tiled=True),
+            jnp.concatenate(
+                lax.all_to_all(
+                    jnp.stack(jnp.split(send_rows, lax.axis_size("dp"), axis=2), axis=0), "dp", 0, 0
+                ),
+                1,
+            ),
             "vocab",
             split_axis=0,
             concat_axis=0,

time: 229 us -> 223 us (0.974)
  waiting for transfers between devices: 82.8 us -> 108 us
  local copies, waits for them, and re-layouts: 24.7 us -> 4.97 us
  blocking collectives: 64 us -> 52 us
    all_gather x1, waiting for transfers between devices: 16.8 us -> 34 us  [body(): lax.all_gather(residual, 'dp', axis=0, tiled=True)]
    all_to_all x1, blocking collectives: 27.8 us -> 15.7 us  [body(): lax.all_to_all(jnp.concatenate(lax.all_to_all(jnp.stack(jnp.split(send_ro...]
    unnamed x12 -> x10, local copies, waits for them, and re-layouts: 13.1 us -> 2.47 us
    all_to_all x1, waiting for transfers between devices: 0.01 us -> 6.35 us  [body(): lax.all_to_all(lax.all_to_all(offset_copies, 'dp', split_axis=2, concat_a...]
    all_to_all x2 -> x1, local copies, waits for them, and re-layouts: 4.98 us -> 0.04 us  [body(): lax.all_to_all(jnp.stack(jnp.split(send_rows, lax.axis_size('dp'), axis=2...]
    all_to_all x1, waiting for transfers between devices: 14.4 us -> 9.44 us  [body(): lax.all_to_all(hidden_full, 'dp', split_axis=1, concat_axis=0, tiled=True)]
    reduce_scatter x1, waiting for transfers between devices: 0.02 us -> 4.41 us  [body(): lax.psum_scatter(hidden_part, 'vocab', scatter_dimension=1, tiled=True)]
    reshape x1 -> x0, local copies, waits for them, and re-layouts: 4.19 us -> none  [body(): send_rows = send_rows.reshape(vocab_count, capacity, model_width)]
  transfers between devices with their start and end apart: 7 -> 7, of which waited for: 4 -> 7; matrix products, arithmetic and copies ran while one was open for 13% -> 5% of each run, Pallas kernels for 0% -> 0%
where the time goes in v1:
time: 223 us
  waiting for transfers between devices  108 us (48%)
  blocking collectives  52 us (23%)
  matrix products  23.9 us (11%)
  between operations  13.9 us (6%)
  starting transfers between devices  13.6 us (6%)
  other arithmetic  6.49 us (3%)
  local copies, waits for them, and re-layouts  4.97 us (2%)
    all_gather x1, waiting for transfers between devices, body(): hidden_full = lax.all_gather(hidden, 'vocab', axis=1, tiled=True)  44 us
    all_gather x1, waiting for transfers between devices, body(): lax.all_gather(residual, 'dp', axis=0, tiled=True)  34 us
    pmax x1, blocking collectives, body(): row_max = lax.pmax(local_max, 'vocab')  19.2 us
    psum x1, blocking collectives, body(): lax.psum((jnp.sum(shifted, axis=1), picked), 'vocab')  17.1 us
    all_to_all x1, blocking collectives, body(): lax.all_to_all(jnp.concatenate(lax.all_to_all(jnp.stack(jnp.split(send_ro...  15.7 us
    all_to_all x1, waiting for transfers between devices, body(): lax.all_to_all(hidden_full, 'dp', split_axis=1, concat_axis=0, tiled=True)  9.44 us
    dot_general x1, matrix products, body(): hidden_part = jnp.dot(residual, table, preferred_element_type=jnp.float32)  7.45 us
    dot_general x1, matrix products, body(): lax.dot_general(lax.all_gather(residual, 'dp', axis=0, tiled=True), hidde...  7 us
  transfers between devices with their start and end apart: 7, of which 7 were waited for; matrix products, arithmetic and copies ran while one was open for 5% of the time, Pallas kernels for 0%

profile of v1, /device:TPU:0, one launch (start us, length us, event | category | flops | bytes accessed | tf_op | source)
XLA Modules:
  0.0 222.9 jit_solution(5920416043830929619)
XLA Ops:
  7.2 0.0 copy-start
  7.2 0.0 all-gather.3.cloned.1.call-start
  7.2 1.7 copy.21
  8.9 0.0 all-gather.3.cloned.1.call-update
  8.9 0.0 reduce-scatter.2.cloned.1.call-start
  9.0 0.7 broadcast_subtract_fusion
  9.7 44.0 %all-gather.3.cloned.1.call-done = bf16[256,2048]{0,1:T(8,128)(2,1)} async-done(((bf16[256,256]{0,1:T(8,128)(2,1)}), bf16[256,2048]{0,1:T(8,128)(2,1)}) %all-gather.3.cloned.1.call-update) | async-done | bytes 1048592 | tf_op jit(solution)/shard_map/all_gather | solution.py:13
  53.7 5.9 %fusion.5 = (f32[256]{0:T(256)S(1)}, f32[256,2000]{0,1:T(8,128)S(1)}) fusion(bf16[2000,2048]{1,0:T(8,128)(2,1)} %param.6, bf16[256,2048]{0,1:T(8,128)(2,1)} %all-gather.3.cloned.1.call-done), kind=kOutput, calls=%fused_computation.27 | convolution fusion | flops 2097663744 | bytes 11289600 | tf_op jit(solution)/shard_map/dot_general | solution.py:14
  59.6 19.2 %pmax.7 = f32[256]{0:T(256)S(1)} all-reduce(f32[256]{0:T(256)S(1)} %get-tuple-element.13), channel_id=1, replica_groups=mesh['dp'=4,'vocab'=8] {'vocab'}, use_global_device_ids=true, to_apply=%region_1.2 | all-reduce | flops 256 | bytes 2048 | tf_op jit(solution)/shard_map/pmax | solution.py:21
  78.7 0.6 fusion.2
  79.3 17.1 %all-reduce = (f32[256]{0:T(256)S(1)}, f32[256]{0:T(256)S(1)}) all-reduce(f32[256]{0:T(256)S(1)} %get-tuple-element.4, f32[256]{0:T(256)S(1)} %get-tuple-element.3), channel_id=1, replica_groups=mesh['dp'=4,'vocab'=8] {'vocab'}, use_global_device_ids=true, to_apply=%region_5.6 | all-reduce | flops 512 | bytes 4096 | tf_op jit(solution)/shard_map/psum | solution.py:23
  96.4 0.6 subtract_convert_fusion
  97.0 0.0 copy-start.1
  97.0 7.5 %fusion.6 = f32[256,2048]{1,0:T(8,128)} fusion(bf16[256,2000]{0,1:T(8,128)(2,1)S(1)} %subtract_convert_fusion, bf16[2000,2048]{1,0:T(8,128)(2,1)} %param.6), kind=kOutput, calls=%fused_computation.30 | convolution fusion | flops 2097152000 | bytes 11313152 | tf_op jit(solution)/shard_map/dot_general | solution.py:26
  104.5 0.0 copy-done.1
  104.5 0.0 copy-start.2
  104.5 0.0 reduce-scatter.2.cloned.1.call-update
  104.5 0.0 all-gather.5.cloned.1.call-start
  104.5 0.7 all-gather.5.cloned.1.call-update
  105.2 0.0 copy-done.2
  105.3 0.2 convert_reduce_fusion
  105.4 0.1 select_reduce_fusion.1
  105.6 0.1 sub.44
  105.6 0.7 reshape.51
  106.3 3.2 %all-to-all-start = ((s32[4,1,128]{2,1,0:T(1,128)}), s32[4,1,128]{2,1,0:T(1,128)S(1)}, u32[]{:S(2)}, u32[]{:S(2)}) async-start(s32[4,1,128]{2,1,0:T(1,128)} %reshape.51), calls=%async_computation.1 | async-start | bytes 4096 | tf_op jit(solution)/shard_map/all_to_all | solution.py:63
  109.5 0.0 copy-done
  109.6 0.4 convolution_convert_fusion
  110.0 0.1 slice_bitcast_fusion.3
  110.0 0.9 pad_maximum_fusion
  110.9 2.3 %all-to-all-done = s32[4,1,128]{2,1,0:T(1,128)S(1)} async-done(((s32[4,1,128]{2,1,0:T(1,128)}), s32[4,1,128]{2,1,0:T(1,128)S(1)}, u32[]{:S(2)}, u32[]{:S(2)}) %all-to-all-start) | async-done | bytes 2080 | tf_op jit(solution)/shard_map/all_to_all | solution.py:63
  113.2 3.5 %all-to-all-start.2 = ((bf16[4,8,16,512]{3,2,1,0:T(8,128)(2,1)}), bf16[4,8,16,512]{3,2,1,0:T(8,128)(2,1)S(1)}, u32[]{:S(2)}, u32[]{:S(2)}) async-start(bf16[4,8,16,512]{3,2,1,0:T(8,128)(2,1)} %pad_maximum_fusion), calls=%async_computation.3 | async-start | bytes 1048576 | tf_op jit(solution)/shard_map/all_to_all | solution.py:52
  116.7 0.5 broadcast.29
  117.2 0.7 reduce.4
  117.9 0.1 reshape.52
  118.0 0.7 all_to_all.39
  118.6 6.8 %all-to-all-done.2 = bf16[4,8,16,512]{3,2,1,0:T(8,128)(2,1)S(1)} async-done(((bf16[4,8,16,512]{3,2,1,0:T(8,128)(2,1)}), bf16[4,8,16,512]{3,2,1,0:T(8,128)(2,1)S(1)}, u32[]{:S(2)}, u32[]{:S(2)}) %all-to-all-start.2) | async-done | bytes 524320 | tf_op jit(solution)/shard_map/all_to_all | solution.py:52
  125.5 3.3 %all-to-all-start.1 = ((s32[8,64,1]{1,2,0:T(1,128)}), s32[8,64,1]{1,2,0:T(1,128)S(1)}, u32[]{:S(2)}, u32[]{:S(2)}) async-start(s32[8,64,1]{1,2,0:T(1,128)} %bitcast.2), calls=%async_computation.2 | async-start | bytes 8192 | tf_op jit(solution)/shard_map/all_to_all | solution.py:62
  128.8 6.4 %all-to-all-done.1 = s32[8,64,1]{1,2,0:T(1,128)S(1)} async-done(((s32[8,64,1]{1,2,0:T(1,128)}), s32[8,64,1]{1,2,0:T(1,128)S(1)}, u32[]{:S(2)}, u32[]{:S(2)}) %all-to-all-start.1) | async-done | bytes 2080 | tf_op jit(solution)/shard_map/all_to_all | solution.py:62
  135.2 15.7 %all_to_all.52 = bf16[8,64,512]{2,1,0:T(8,128)(2,1)S(1)} all-to-all(bf16[8,64,512]{2,1,0:T(8,128)(2,1)S(1)} %bitcast.37), channel_id=1, replica_groups=mesh['dp'=4,'vocab'=8] {'vocab'}, dimensions={0} | all-to-all | bytes 1048576 | tf_op jit(solution)/shard_map/all_to_all | solution.py:50
  150.9 3.5 %all-to-all-start.4 = ((bf16[256,4,512]{0,2,1:T(8,128)(2,1)}), bf16[256,4,512]{0,2,1:T(8,128)(2,1)S(1)}, u32[]{:S(2)}, u32[]{:S(2)}) async-start(bf16[256,4,512]{0,2,1:T(8,128)(2,1)} %bitcast.11), calls=%async_computation.5 | async-start | bytes 2097152 | tf_op jit(solution)/shard_map/all_to_all | solution.py:78
  154.4 0.5 broadcast.27
  154.9 0.7 reduce.3
  155.6 0.1 eq.46
  155.7 3.1 %fusion = f32[2000,512]{1,0:T(8,128)} fusion(bf16[512,512]{1,0:T(8,128)(2,1)S(1)} %bitcast.40, s32[512]{0:T(512)S(1)} %eq.46), kind=kOutput, calls=%fused_computation.2 | convolution fusion | flops 1049600000 | bytes 4622336 | tf_op jit(solution)/shard_map/dot_general | solution.py:77
  158.8 0.6 add_subtract_fusion
  159.4 9.4 %all-to-all-done.4 = bf16[256,4,512]{0,2,1:T(8,128)(2,1)S(1)} async-done(((bf16[256,4,512]{0,2,1:T(8,128)(2,1)}), bf16[256,4,512]{0,2,1:T(8,128)(2,1)S(1)}, u32[]{:S(2)}, u32[]{:S(2)}) %all-to-all-start.4) | async-done | bytes 1048608 | tf_op jit(solution)/shard_map/all_to_all | solution.py:78
  168.8 0.5 copy.25
  169.4 4.4 %reduce-scatter.2.cloned.1.call-done = f32[256,256]{1,0:T(8,128)} async-done(((f32[256,2048]{1,0:T(8,128)}), f32[256,256]{1,0:T(8,128)}) %reduce-scatter.2.cloned.1.call-update) | async-done | bytes 262160 | tf_op jit(solution)/shard_map/reduce_scatter | solution.py:27
  173.8 1.6 convert_element_type.18
  175.4 34.0 %all-gather.5.cloned.1.call-done = bf16[1024,2000]{0,1:T(8,128)(2,1)} async-done(((bf16[256,2000]{0,1:T(8,128)(2,1)}), bf16[1024,2000]{0,1:T(8,128)(2,1)}) %all-gather.5.cloned.1.call-update) | async-done | bytes 4096016 | tf_op jit(solution)/shard_map/all_gather | solution.py:80
  209.4 7.0 %add_convert_fusion = bf16[2000,512]{1,0:T(8,128)(2,1)} fusion(f32[2000,512]{1,0:T(8,128)} %fusion, bf16[1024,2000]{0,1:T(8,128)(2,1)} %all-gather.5.cloned.1.call-done, bf16[1024,512]{1,0:T(8,128)(2,1)S(1)} %bitcast.39), kind=kOutput, calls=%fused_computation | convolution fusion | flops 2099200000 | bytes 11288576 | tf_op jit(solution)/shard_map/dot_general | solution.py:79
  (7 shorter events, 0.1 us)
Async XLA Ops:
  7.2 102.4 %copy-start = (bf16[64,2048]{1,0:T(8,128)(2,1)S(1)}, bf16[64,2048]{1,0:T(8,128)(2,1)}, u32[]{:S(2)}) copy-start(bf16[64,2048]{1,0:T(8,128)(2,1)} %param.9) | copy-start | bytes 786436
  7.2 46.5 %all-gather.3.cloned.1.call-start = ((), (), s32[]{:S(2)}) async-start(), calls=%async_computation.6 | async-start | bytes 1179648 | tf_op jit(solution)/shard_map/all_gather | solution.py:13
  8.9 164.8 %reduce-scatter.2.cloned.1.call-start = ((), (), s32[]{:S(2)}) async-start(), calls=%async_computation.7 | async-start | bytes 2359296 | tf_op jit(solution)/shard_map/reduce_scatter | solution.py:27
  97.0 7.5 %copy-start.1 = (bf16[256,2000]{0,1:T(8,128)(2,1)}, bf16[256,2000]{0,1:T(8,128)(2,1)S(1)}, u32[]{:S(2)}) copy-start(bf16[256,2000]{0,1:T(8,128)(2,1)S(1)} %subtract_convert_fusion) | copy-start | bytes 3072004
  104.5 0.8 copy-start.2
  104.5 104.9 %all-gather.5.cloned.1.call-start = ((), (), s32[]{:S(2)}) async-start(), calls=%async_computation.8 | async-start | bytes 5120000 | tf_op jit(solution)/shard_map/all_gather | solution.py:80
  106.3 6.9 %all-to-all-start = ((s32[4,1,128]{2,1,0:T(1,128)}), s32[4,1,128]{2,1,0:T(1,128)S(1)}, u32[]{:S(2)}, u32[]{:S(2)}) async-start(s32[4,1,128]{2,1,0:T(1,128)} %reshape.51), calls=%async_computation.1 | async-start | bytes 4096 | tf_op jit(solution)/shard_map/all_to_all | solution.py:63
  113.2 12.3 %all-to-all-start.2 = ((bf16[4,8,16,512]{3,2,1,0:T(8,128)(2,1)}), bf16[4,8,16,512]{3,2,1,0:T(8,128)(2,1)S(1)}, u32[]{:S(2)}, u32[]{:S(2)}) async-start(bf16[4,8,16,512]{3,2,1,0:T(8,128)(2,1)} %pad_maximum_fusion), calls=%async_computation.3 | async-start | bytes 1048576 | tf_op jit(solution)/shard_map/all_to_all | solution.py:52
  125.5 9.7 %all-to-all-start.1 = ((s32[8,64,1]{1,2,0:T(1,128)}), s32[8,64,1]{1,2,0:T(1,128)S(1)}, u32[]{:S(2)}, u32[]{:S(2)}) async-start(s32[8,64,1]{1,2,0:T(1,128)} %bitcast.2), calls=%async_computation.2 | async-start | bytes 8192 | tf_op jit(solution)/shard_map/all_to_all | solution.py:62
  150.9 17.9 %all-to-all-start.4 = ((bf16[256,4,512]{0,2,1:T(8,128)(2,1)}), bf16[256,4,512]{0,2,1:T(8,128)(2,1)S(1)}, u32[]{:S(2)}, u32[]{:S(2)}) async-start(bf16[256,4,512]{0,2,1:T(8,128)(2,1)} %bitcast.11), calls=%async_computation.5 | async-start | bytes 2097152 | tf_op jit(solution)/shard_map/all_to_all | solution.py:78
Sparse Core Ops, SparseCore 0:
  10.7 42.9 all-gather.2
  104.6 69.1 reduce-scatter.1
  175.9 33.4 all-gather.4
